TPU v7x, 32 devices: a whole 2x2x4 slice. The times are simulated.
32 devices in a mesh: dp: 8 (over z, x), tp: 4 (over y, core).
Axes of the slice: x: 2, y: 2, z: 4, core: 2. Of those that a mesh axis runs over, the one named last changes fastest.
Arguments:
- main: bfloat16 [16512, 1152], P('dp', 'tp'), may hold values from -6 to 6
- long_skip: bfloat16 [16512, 1152], P('dp', 'tp'), may hold values from -6 to 6
- cotangent: bfloat16 [16512, 1152], P('dp', 'tp'), may hold values from -6 to 6
- timesteps: int32 [64], P('dp'), may hold values from 0 to 999
- loss_codes: int32 [64], P('dp'), may hold values from 0 to 7
- code_weights: float32 [8], replicated, may hold values from 0.25 to 4
- item_counts: int32 [8], P('dp'), may hold values from 4 to 8, as said below
- w_skip_main: bfloat16 [1152, 1152], P('tp'), may hold values from -0.125 to 0.125
- w_skip_long: bfloat16 [1152, 1152], P('tp'), may hold values from -0.125 to 0.125
- b_skip: float32 [1152], P('tp'), may hold values from -3 to 3
- ln1_gain: float32 [1152], P('tp'), may hold values from 0.25 to 1.75
- ln1_bias: float32 [1152], P('tp'), may hold values from -2.4 to 2.4
- w_qkv: bfloat16 [3, 1152, 1152], P(None, None, 'tp'), may hold values from -0.1875 to 0.1875
- w_proj: bfloat16 [1152, 1152], P('tp'), may hold values from -1.5 to 1.5
- b_proj: float32 [1152], P('tp'), may hold values from -3 to 3
- ln2_gain: float32 [1152], P('tp'), may hold values from 0.25 to 1.75
- ln2_bias: float32 [1152], P('tp'), may hold values from -2.4 to 2.4
- w_up: bfloat16 [1152, 4608], P(None, 'tp'), may hold values from -0.1875 to 0.1875
- b_up: float32 [4608], P('tp'), may hold values from -3 to 3
- w_down: bfloat16 [4608, 1152], P('tp'), may hold values from -0.09375 to 0.09375
- b_down: float32 [1152], P('tp'), may hold values from -3 to 3
Outputs:
- out: bfloat16 [16512, 1152], P('dp', 'tp')
- d_main: bfloat16 [16512, 1152], P('dp', 'tp')
- d_long: bfloat16 [16512, 1152], P('dp', 'tp')
- g_w_skip_main: float32 [1152, 1152], P('tp')
- g_w_skip_long: float32 [1152, 1152], P('tp')
- g_b_skip: float32 [1152], P('tp')
- g_ln1_gain: float32 [1152], P('tp')
- g_ln1_bias: float32 [1152], P('tp')
- g_w_qkv: float32 [3, 1152, 1152], P(None, None, 'tp')
- g_w_proj: float32 [1152, 1152], P('tp')
- g_b_proj: float32 [1152], P('tp')
- g_ln2_gain: float32 [1152], P('tp')
- g_ln2_bias: float32 [1152], P('tp')
- g_w_up: float32 [1152, 4608], P(None, 'tp')
- g_b_up: float32 [4608], P('tp')
- g_w_down: float32 [4608, 1152], P('tp')
- g_b_down: float32 [1152], P('tp')
Inputs may be any that keep to these rules, and one draw needn't show every extreme that they name: `item_counts`: each batch group holds 4 to 8 items; some group is full and some holds exactly 4.
All inputs are finite; a program needn't handle non-finite values.
Results may differ from a plain program's by a relative error of at most 0.02.
Values may be sent and summed in bfloat16 or wider, within the bound.
A program may use at most 192 MiB of HBM per device.

v0:
```python
import math
import jax
import jax.numpy as jnp
from jax import lax
from jax.sharding import PartitionSpec as P

HEAD = 72
SEQ = 258
TSTEPS = 1000
EPSILON = 1e-06
ROOT_HALF = 0.7071067811865476
DENSITY_SCALE = 0.3989422804014327


def item_factors(timesteps, loss_codes, code_weights, group_items):
    steps_float = timesteps.astype(jnp.float32)
    phase = (steps_float / TSTEPS + 0.008) / 1.008 * (math.pi / 2.0)
    cosine = jnp.cos(phase)
    signal = cosine * cosine
    weight = jnp.minimum(1.0, 5.0 * (1.0 - signal) / signal)
    picks = (
        loss_codes[:, None] == jnp.arange(code_weights.shape[0], dtype=jnp.int32)[None, :]
    ).astype(jnp.float32)
    coded = jnp.sum(picks * code_weights[None, :], axis=1)
    valid = (jnp.arange(timesteps.shape[0], dtype=jnp.int32) < group_items).astype(jnp.float32)
    return (weight * coded * valid, valid)


def layer_norm(stream, gain, bias, width):
    totals, squares = lax.psum((jnp.sum(stream, 0), jnp.sum(stream * stream, 0)), "tp")
    mean = totals / width
    rstd = lax.rsqrt(squares / width - mean * mean + EPSILON)
    normed = (stream - mean[None, :]) * rstd[None, :]
    rounded = (normed * gain[:, None] + bias[:, None]).astype(jnp.bfloat16)
    return (normed, rstd, lax.all_gather(rounded, "tp", axis=0, tiled=True))


def norm_back(d_normed, normed, rstd, gain, width):
    g_gain = jnp.sum(d_normed * normed, 1)
    g_bias = jnp.sum(d_normed, 1)
    scaled = d_normed * gain[:, None]
    first, second = lax.psum((jnp.sum(scaled, 0), jnp.sum(scaled * normed, 0)), "tp")
    back = rstd[None, :] * (scaled - first[None, :] / width - normed * second[None, :] / width)
    return (back, g_gain, g_bias)


def reduce_back(term, local_width):
    return lax.psum_scatter(
        term(jnp.int32(0), lax.axis_size("tp") * local_width).astype(jnp.bfloat16),
        "tp",
        scatter_dimension=0,
        tiled=True,
    ).astype(jnp.float32)


def fold_back(shard, pairs):
    piece = lax.all_gather(shard, "tp", axis=0, tiled=True)
    new_acts = tuple(
        (
            jnp.einsum("fc,ct->ft", weight, piece, preferred_element_type=jnp.float32)
            for weight, acts in pairs
        )
    )
    new_weights = tuple(
        (
            jnp.einsum("ft,ct->fc", acts, piece, preferred_element_type=jnp.float32)
            for weight, acts in pairs
        )
    )
    return (new_acts, new_weights)


def split_heads(flat, heads_here):
    pair_count = flat.shape[1] // (2 * SEQ)
    shaped = flat.reshape(heads_here, HEAD, pair_count, 2, SEQ)
    return jnp.moveaxis(shaped, 2, 0)


def join_heads(blocks):
    moved = jnp.moveaxis(blocks, 0, 2)
    return moved.reshape(moved.shape[0] * moved.shape[1], -1)


def attend(block):
    query_rows, key_rows, value_rows = block
    scale = 1.0 / math.sqrt(HEAD)
    scores = (
        jnp.einsum("hdbi,hdbj->hbij", query_rows, key_rows, preferred_element_type=jnp.float32)
        * scale
    )
    peak = jnp.max(scores, axis=-1, keepdims=True)
    logsum = peak + jnp.log(jnp.sum(jnp.exp(scores - peak), axis=-1, keepdims=True))
    probs = jnp.exp(scores - logsum).astype(jnp.bfloat16)
    attended = jnp.einsum("hbij,hdbj->hdbi", probs, value_rows, preferred_element_type=jnp.float32)
    return (attended.astype(jnp.bfloat16), logsum[..., 0])


def attend_back(block):
    query_rows, key_rows, value_rows, logsum, d_attended = block
    scale = 1.0 / math.sqrt(HEAD)
    scores = (
        jnp.einsum("hdbi,hdbj->hbij", query_rows, key_rows, preferred_element_type=jnp.float32)
        * scale
    )
    probs = jnp.exp(scores - logsum[..., None])
    probs_low = probs.astype(jnp.bfloat16)
    d_probs = jnp.einsum(
        "hdbi,hdbj->hbij", d_attended, value_rows, preferred_element_type=jnp.float32
    )
    delta = jnp.sum(probs * d_probs, axis=-1, keepdims=True)
    d_scores = (probs * (d_probs - delta)).astype(jnp.bfloat16)
    d_query = (
        jnp.einsum("hbij,hdbj->hdbi", d_scores, key_rows, preferred_element_type=jnp.float32)
        * scale
    )
    d_key = (
        jnp.einsum("hbij,hdbi->hdbj", d_scores, query_rows, preferred_element_type=jnp.float32)
        * scale
    )
    d_value = jnp.einsum(
        "hbij,hdbi->hdbj", probs_low, d_attended, preferred_element_type=jnp.float32
    )
    return (d_query.astype(jnp.bfloat16), d_key.astype(jnp.bfloat16), d_value.astype(jnp.bfloat16))


def body(
    main,
    long_skip,
    cotangent,
    timesteps,
    loss_codes,
    code_weights,
    item_counts,
    w_skip_main,
    w_skip_long,
    b_skip,
    ln1_gain,
    ln1_bias,
    w_qkv,
    w_proj,
    b_proj,
    ln2_gain,
    ln2_bias,
    w_up,
    b_up,
    w_down,
    b_down,
):
    local_width = main.shape[1]
    width = w_skip_main.shape[1]
    heads_here = local_width // HEAD
    item_scale, valid = item_factors(timesteps, loss_codes, code_weights, item_counts[0])
    row_scale = jnp.repeat(item_scale, SEQ)
    row_valid = jnp.repeat(valid, SEQ)
    main_cols = main.T
    long_cols = long_skip.T
    stream = (
        lax.psum_scatter(
            jnp.einsum("dc,dt->ct", w_skip_main, main_cols, preferred_element_type=jnp.float32)
            + jnp.einsum("dc,dt->ct", w_skip_long, long_cols, preferred_element_type=jnp.float32),
            "tp",
            scatter_dimension=0,
            tiled=True,
        )
        + b_skip[:, None]
    )
    normed_one, rstd_one, full_one = layer_norm(stream, ln1_gain, ln1_bias, width)
    qkv = jnp.einsum("edc,dt->ect", w_qkv, full_one, preferred_element_type=jnp.float32).astype(
        jnp.bfloat16
    )
    query_blocks = split_heads(qkv[0], heads_here)
    key_blocks = split_heads(qkv[1], heads_here)
    value_blocks = split_heads(qkv[2], heads_here)
    attended_blocks, logsums = lax.map(attend, (query_blocks, key_blocks, value_blocks))
    attended = join_heads(attended_blocks)
    cols_here = w_proj
    projected = lax.psum_scatter(
        jnp.einsum("rc,rt->ct", cols_here, attended, preferred_element_type=jnp.float32).astype(
            jnp.bfloat16
        ),
        "tp",
        scatter_dimension=0,
        tiled=True,
    ).astype(jnp.float32)
    stream_two = stream + projected + b_proj[:, None]
    normed_two, rstd_two, full_two = layer_norm(stream_two, ln2_gain, ln2_bias, width)
    upward = (
        jnp.einsum("dc,dt->ct", w_up, full_two, preferred_element_type=jnp.float32) + b_up[:, None]
    )
    activated = jax.nn.gelu(upward, approximate=False).astype(jnp.bfloat16)
    cols_here = w_down
    result = (
        stream_two
        + lax.psum_scatter(
            jnp.einsum(
                "fc,ft->ct", cols_here, activated, preferred_element_type=jnp.float32
            ).astype(jnp.bfloat16),
            "tp",
            scatter_dimension=0,
            tiled=True,
        ).astype(jnp.float32)
        + b_down[:, None]
    )
    out = (result * row_valid[None, :]).T.astype(jnp.bfloat16)
    grad_low = (cotangent.T.astype(jnp.float32) * row_scale[None, :]).astype(jnp.bfloat16)
    grad_wide = grad_low.astype(jnp.float32)
    g_b_down = jnp.sum(grad_wide, 1)
    (d_activated,), (g_w_down,) = fold_back(grad_low, ((w_down, activated),))
    cumulative = 0.5 * (1.0 + lax.erf(upward * ROOT_HALF))
    density = jnp.exp(-0.5 * upward * upward) * DENSITY_SCALE
    d_upward = (d_activated * (cumulative + upward * density)).astype(jnp.bfloat16)
    g_b_up = jnp.sum(d_upward.astype(jnp.float32), 1)
    g_w_up = jnp.einsum("dt,ft->df", full_two, d_upward, preferred_element_type=jnp.float32)

    def up_term(start, count_rows):
        return jnp.einsum("cf,ft->ct", w_up, d_upward, preferred_element_type=jnp.float32)

    d_normed_two = reduce_back(up_term, local_width)
    back_two, g_ln2_gain, g_ln2_bias = norm_back(
        d_normed_two, normed_two, rstd_two, ln2_gain, width
    )
    d_stream_two = (back_two + grad_wide).astype(jnp.bfloat16)
    d_stream_wide = d_stream_two.astype(jnp.float32)
    g_b_proj = jnp.sum(d_stream_wide, 1)
    (d_attended,), (g_w_proj,) = fold_back(d_stream_two, ((w_proj, attended),))
    d_attended_blocks = split_heads(d_attended.astype(jnp.bfloat16), heads_here)
    d_queries, d_keys, d_values = lax.map(
        attend_back, (query_blocks, key_blocks, value_blocks, logsums, d_attended_blocks)
    )
    d_qkv = jnp.stack([join_heads(d_queries), join_heads(d_keys), join_heads(d_values)], axis=0)
    g_w_qkv = jnp.einsum("dt,ect->edc", full_one, d_qkv, preferred_element_type=jnp.float32)

    def qkv_term(start, count_rows):
        return jnp.einsum("ecr,ert->ct", w_qkv, d_qkv, preferred_element_type=jnp.float32)

    d_normed_one = reduce_back(qkv_term, local_width)
    back_one, g_ln1_gain, g_ln1_bias = norm_back(
        d_normed_one, normed_one, rstd_one, ln1_gain, width
    )
    d_stream = (back_one + d_stream_wide).astype(jnp.bfloat16)
    g_b_skip = jnp.sum(d_stream.astype(jnp.float32), 1)
    (d_main_cols, d_long_cols), (g_w_main, g_w_long) = fold_back(
        d_stream, ((w_skip_main, main_cols), (w_skip_long, long_cols))
    )
    (
        g_w_main,
        g_w_long,
        g_b_skip,
        g_ln1_gain,
        g_ln1_bias,
        g_w_qkv,
        g_w_proj,
        g_b_proj,
        g_ln2_gain,
        g_ln2_bias,
        g_w_up,
        g_b_up,
        g_w_down,
        g_b_down,
    ) = (
        lax.psum(g_w_main.astype(jnp.bfloat16), "dp").astype(jnp.float32),
        lax.psum(g_w_long.astype(jnp.bfloat16), "dp").astype(jnp.float32),
        lax.psum(g_b_skip.astype(jnp.bfloat16), "dp").astype(jnp.float32),
        lax.psum(g_ln1_gain.astype(jnp.bfloat16), "dp").astype(jnp.float32),
        lax.psum(g_ln1_bias.astype(jnp.bfloat16), "dp").astype(jnp.float32),
        lax.psum(g_w_qkv.astype(jnp.bfloat16), "dp").astype(jnp.float32),
        lax.psum(g_w_proj.astype(jnp.bfloat16), "dp").astype(jnp.float32),
        lax.psum(g_b_proj.astype(jnp.bfloat16), "dp").astype(jnp.float32),
        lax.psum(g_ln2_gain.astype(jnp.bfloat16), "dp").astype(jnp.float32),
        lax.psum(g_ln2_bias.astype(jnp.bfloat16), "dp").astype(jnp.float32),
        lax.psum(g_w_up.astype(jnp.bfloat16), "dp").astype(jnp.float32),
        lax.psum(g_b_up.astype(jnp.bfloat16), "dp").astype(jnp.float32),
        lax.psum(g_w_down.astype(jnp.bfloat16), "dp").astype(jnp.float32),
        lax.psum(g_b_down.astype(jnp.bfloat16), "dp").astype(jnp.float32),
    )
    d_main = d_main_cols.T.astype(jnp.bfloat16)
    d_long = d_long_cols.T.astype(jnp.bfloat16)
    return (
        out,
        d_main,
        d_long,
        g_w_main,
        g_w_long,
        g_b_skip,
        g_ln1_gain,
        g_ln1_bias,
        g_w_qkv,
        g_w_proj,
        g_b_proj,
        g_ln2_gain,
        g_ln2_bias,
        g_w_up,
        g_b_up,
        g_w_down,
        g_b_down,
    )


def solution(mesh):
    return jax.shard_map(
        body,
        mesh=mesh,
        in_specs=(
            P("dp", "tp"),
            P("dp", "tp"),
            P("dp", "tp"),
            P("dp"),
            P("dp"),
            P(),
            P("dp"),
            P("tp", None),
            P("tp", None),
            P("tp"),
            P("tp"),
            P("tp"),
            P(None, None, "tp"),
            P("tp", None),
            P("tp"),
            P("tp"),
            P("tp"),
            P(None, "tp"),
            P("tp"),
            P("tp", None),
            P("tp"),
        ),
        out_specs=(
            P("dp", "tp"),
            P("dp", "tp"),
            P("dp", "tp"),
            P("tp", None),
            P("tp", None),
            P("tp"),
            P("tp"),
            P("tp"),
            P(None, None, "tp"),
            P("tp", None),
            P("tp"),
            P("tp"),
            P("tp"),
            P(None, "tp"),
            P("tp"),
            P("tp", None),
            P("tp"),
        ),
        check_vma=False,
    )
```

profile of v0, /device:TPU:0, one launch (start us, length us, event | category | flops | bytes accessed | tf_op | source)
XLA Modules:
  0.0 1135.2 jit_solution(10548227006924629064)
XLA Ops:
  11.9 6.9 convolution_add_fusion
  18.9 84.4 %reduce-scatter.16.cloned.1.call-done = f32[288,2064]{1,0:T(8,128)} async-done(((f32[1152,2064]{1,0:T(8,128)}), f32[288,2064]{1,0:T(8,128)}) %reduce-scatter.16.cloned.1.call-update) | async-done | bytes 2377744
  109.4 10.3 all-reduce.3
  126.7 39.5 %all-gather.6.cloned.1.call-done = bf16[1152,2064]{1,0:T(8,128)(2,1)} async-done(((bf16[288,2064]{1,0:T(8,128)(2,1)}), bf16[1152,2064]{1,0:T(8,128)(2,1)}) %all-gather.6.cloned.1.call-update) | async-done | bytes 4755472 | tf_op jit(solution)/shard_map/all_gather | solution.py:35
  166.2 8.2 fusion.83
  176.4 6.6 reshape_squeeze.11
  183.0 6.6 reshape_squeeze.10
  203.0 23.4 %while.26 = (s32[]{:T(128)}, bf16[4,4,72,2,258]{4,2,3,1,0:T(8,128)(2,1)}, f32[4,4,2,258]{3,2,1,0:T(2,128)}, bf16[4,4,72,2,258]{4,2,3,1,0:T(8,128)(2,1)}, bf16[4,...) while((s32[]{:T(128)}, bf16[4,4,72,2,258]{4,2,3,1,0:T(8,128)(2,1)}, ...), condition=%wide.region_8.0_spmd, body=%wide.region_5.8_spmd.sunk | while | flops 157770096 | bytes 8231833 | solution.py:174
  242.0 8.4 copy.129
  250.5 50.0 %reduce-scatter.18.cloned.1.call-done = bf16[288,2064]{1,0:T(8,128)(2,1)} async-done(((bf16[1152,2064]{1,0:T(8,128)(2,1)}), bf16[288,2064]{1,0:T(8,128)(2,1)}) %reduce-scatter.18.cloned.1.call-update) | async-done | bytes 1188880
  307.6 10.3 all-reduce.2
  333.6 30.3 %all-gather.8.cloned.1.call-done = bf16[1152,2064]{1,0:T(8,128)(2,1)} async-done(((bf16[288,2064]{1,0:T(8,128)(2,1)}), bf16[1152,2064]{1,0:T(8,128)(2,1)}) %all-gather.8.cloned.1.call-update) | async-done | bytes 4755472 | tf_op jit(solution)/shard_map/all_gather | solution.py:35
  363.9 32.2 %fusion.68 = (bf16[1152,2064]{0,1:T(8,128)(2,1)S(1)}, f32[1152,2064]{0,1:T(8,128)}) fusion(f32[1152]{0:T(1024)S(1)} %copy-done.46, bf16[1152,2064]{1,0:T(8,128)(2,1)} %all-gather.8.cloned.1.call-done, bf16[1152,1152]{1,0:T(8,128)(2,1)S(1)} %copy-done), kind=kOutput, calls=%fused_computation.81 | convolution fusion | flops 5635215360 | bytes 21680640 | tf_op jit(solution)/shard_map/dc,dt->ct/dot_general | solution.py:188
  398.4 8.5 fusion.63
  406.9 8.4 copy.131
  415.3 16.6 %fusion.122 = (bf16[1152]{0:T(1024)(128)(2,1)}, bf16[1152,2064]{0,1:T(8,128)(2,1)S(1)}) fusion(f32[1152,2064]{0,1:T(8,128)} %get-tuple-element.220, bf16[1152,2064]{1,0:T(8,128)(2,1)} %all-gather.10.cloned.1.call-done, bf16[1152,1152]{1,0:T(8,128)(2,1)} %param.44), kind=kOutput, calls=%fused_computation.176 | convolution fusion | flops 5504439296 | bytes 21678336 | tf_op jit(solution)/shard_map/fc,ct->ft/dot_general | solution.py:60
  434.1 8.7 fusion.64
  442.8 8.4 copy.133
  451.4 13.8 %reduce-scatter.20.cloned.1.call-done = bf16[288,2064]{1,0:T(8,128)(2,1)} async-done(((bf16[1152,2064]{1,0:T(8,128)(2,1)}), bf16[288,2064]{1,0:T(8,128)(2,1)}) %reduce-scatter.20.cloned.1.call-update) | async-done | bytes 1188880
  467.8 50.5 %reduce-scatter.22.cloned.1.call-done = bf16[288,2064]{1,0:T(8,128)(2,1)} async-done(((bf16[1152,2064]{1,0:T(8,128)(2,1)}), bf16[288,2064]{1,0:T(8,128)(2,1)}) %reduce-scatter.22.cloned.1.call-update) | async-done | bytes 1188880
  526.9 10.3 all-reduce.1
  544.9 39.8 %all-gather.12.cloned.1.call-done = bf16[1152,2064]{1,0:T(8,128)(2,1)} async-done(((bf16[288,2064]{1,0:T(8,128)(2,1)}), bf16[1152,2064]{1,0:T(8,128)(2,1)}) %all-gather.12.cloned.1.call-update) | async-done | bytes 4755472 | tf_op jit(solution)/shard_map/all_gather | solution.py:57
  601.7 51.3 %while.27 = (s32[]{:T(128)}, bf16[4,4,72,2,258]{4,2,3,1,0:T(8,128)(2,1)}, bf16[4,4,72,2,258]{4,2,3,1,0:T(8,128)(2,1)}, bf16[4,4,72,2,258]{4,2,3,1,0:T(8,128)(2,1...) while((s32[]{:T(128)}, ...), condition=%wide.region_23.24_spmd, body=%wide.region_21.23_spmd.sunk | while | flops 390539744 | bytes 20462064 | solution.py:227
  678.8 7.7 fusion.65
  686.5 8.4 copy.135
  695.0 50.0 %reduce-scatter.24.cloned.1.call-done = bf16[288,2064]{1,0:T(8,128)(2,1)} async-done(((bf16[1152,2064]{1,0:T(8,128)(2,1)}), bf16[288,2064]{1,0:T(8,128)(2,1)}) %reduce-scatter.24.cloned.1.call-update) | async-done | bytes 1188880
  751.9 10.5 all-reduce
  770.1 11.5 %convolution_convert_fusion.4 = bf16[1152,1152]{1,0:T(8,128)(2,1)} fusion(bf16[1152,2064]{1,0:T(8,128)(2,1)} %all-gather.8.cloned.1.call-done, bf16[1152,2064]{0,1:T(8,128)(2,1)} %copy-done.49), kind=kOutput, calls=%fused_computation.102 | convolution fusion | flops 5479612416 | bytes 12165120 | tf_op jit(solution)/shard_map/dt,ft->df/dot_general | solution.py:213
  781.6 12.4 %convolution_convert_fusion.3 = bf16[1152,1152]{1,0:T(8,128)(2,1)} fusion(bf16[1152,2064]{0,1:T(8,128)(2,1)} %copy-done.50, bf16[1152,2064]{1,0:T(8,128)(2,1)} %all-gather.10.cloned.1.call-done), kind=kOutput, calls=%fused_computation.101 | convolution fusion | flops 5479612416 | bytes 12165120 | tf_op jit(solution)/shard_map/ft,ct->fc/dot_general | solution.py:66
  796.9 6.9 fusion.108
  823.3 39.2 %all-reduce.4 = (bf16[288]{0:T(512)(128)(2,1)S(1)}, bf16[288]{0:T(512)(128)(2,1)S(1)}, bf16[288]{0:T(512)(128)(2,1)S(1)}, bf16[288]{0:T(512)(128)(2,1)S(1)}, bf1...) all-reduce(bf16[288]{0:T(512)(128)(2,1)S(1)} %get-tuple-element.204, ...), channel_id=1, replica_groups=mesh['dp'=8,'tp'=4] {'dp'}, use_global_device_ids=true, to_apply=%region_32.33 | all-reduce | flops 3168 | bytes 12672 | tf_op jit(solution)/shard_map/psum | solution.py:263
  877.9 235.9 %all-reduce.8.cloned.1.call-done = (bf16[288,1152]{1,0:T(8,128)(2,1)}, bf16[288,1152]{1,0:T(8,128)(2,1)}, bf16[3,1152,288]{1,2,0:T(8,128)(2,1)}, bf16[288,1152]{...) async-done(((bf16[288,1152]{1,0:T(8,128)(2,1)}, bf16[288,1152]{1,0:T(8,128)(2,1)}, bf16[3,1152,288]{1,2,0:T(8,128)(2,1)}, ...) | async-done | bytes 9289744 | tf_op jit(solution)/shard_map/psum | solution.py:261
  (259 shorter events, 278.4 us)
Async XLA Ops:
  7.2 356.7 %copy-start = (bf16[1152,1152]{1,0:T(8,128)(2,1)S(1)}, bf16[1152,1152]{1,0:T(8,128)(2,1)}, u32[]{:S(2)}) copy-start(bf16[1152,1152]{1,0:T(8,128)(2,1)} %param.42) | copy-start | bytes 7962628
  7.2 96.1 %reduce-scatter.16.cloned.1.call-start = ((), (), s32[]{:S(2)}) async-start(), calls=%async_computation.10 | async-start | bytes 12533760
  18.8 88.0 %copy-start.30 = (f32[288]{0:T(512)S(1)}, f32[288]{0:T(512)}, u32[]{:S(2)}) copy-start(f32[288]{0:T(512)} %param.34) | copy-start | bytes 3460
  18.8 101.5 %copy-start.33 = (f32[288]{0:T(512)S(1)}, f32[288]{0:T(512)}, u32[]{:S(2)}) copy-start(f32[288]{0:T(512)} %param.35) | copy-start | bytes 3460
  18.9 101.5 %copy-start.36 = (f32[288]{0:T(512)S(1)}, f32[288]{0:T(512)}, u32[]{:S(2)}) copy-start(f32[288]{0:T(512)} %param.36) | copy-start | bytes 3460
  18.9 147.4 %all-gather.6.cloned.1.call-start = ((), (), s32[]{:S(2)}) async-start(), calls=%async_computation.5 | async-start | bytes 6266880 | tf_op jit(solution)/shard_map/all_gather | solution.py:35
  126.4 174.0 %reduce-scatter.18.cloned.1.call-start = ((), (), s32[]{:S(2)}) async-start(), calls=%async_computation.11 | async-start | bytes 6266880
  250.4 52.6 %copy-start.37 = (f32[288]{0:T(512)S(1)}, f32[288]{0:T(512)}, u32[]{:S(2)}) copy-start(f32[288]{0:T(512)} %param.39) | copy-start | bytes 3460
  250.4 113.5 %all-gather.8.cloned.1.call-start = ((), (), s32[]{:S(2)}) async-start(), calls=%async_computation.6 | async-start | bytes 6266880 | tf_op jit(solution)/shard_map/all_gather | solution.py:35
  303.0 14.9 %copy-start.32 = (f32[288]{0:T(512)S(1)}, f32[288]{0:T(512)}, u32[]{:S(2)}) copy-start(f32[288]{0:T(512)} %param.40) | copy-start | bytes 3460
  303.0 14.9 %copy-start.38 = (f32[288]{0:T(512)S(1)}, f32[288]{0:T(512)}, u32[]{:S(2)}) copy-start(f32[288]{0:T(512)} %param.41) | copy-start | bytes 3460
  324.0 91.3 %all-gather.10.cloned.1.call-start = ((), (), s32[]{:S(2)}) async-start(), calls=%async_computation.7 | async-start | bytes 6266880 | tf_op jit(solution)/shard_map/all_gather | solution.py:57
  328.0 35.9 %copy-start.46 = (f32[1152]{0:T(1024)S(1)}, f32[1152]{0:T(1024)}, u32[]{:S(2)}) copy-start(f32[1152]{0:T(1024)} %param.43) | copy-start | bytes 13828
  333.6 131.7 %reduce-scatter.20.cloned.1.call-start = ((), (), s32[]{:S(2)}) async-start(), calls=%async_computation.12 | async-start | bytes 6266880
  363.9 34.5 %copy-start.42 = (bf16[1152,1152]{1,0:T(8,128)(2,1)S(1)}, bf16[1152,1152]{1,0:T(8,128)(2,1)}, u32[]{:S(2)}) copy-start(bf16[1152,1152]{1,0:T(8,128)(2,1)} %param.44) | copy-start | bytes 7962628
  415.3 103.1 %reduce-scatter.22.cloned.1.call-start = ((), (), s32[]{:S(2)}) async-start(), calls=%async_computation.13 | async-start | bytes 6266880
  451.2 69.7 %copy-start.39 = (f32[288]{0:T(512)S(1)}, f32[288]{0:T(512)}, u32[]{:S(2)}) copy-start(f32[288]{0:T(512)} %param.45) | copy-start | bytes 3460
  451.2 133.4 %all-gather.12.cloned.1.call-start = ((), (), s32[]{:S(2)}) async-start(), calls=%async_computation.8 | async-start | bytes 6266880 | tf_op jit(solution)/shard_map/all_gather | solution.py:57
  520.9 16.3 %copy-start.2 = (bf16[2064,288]{1,0:T(8,128)(2,1)S(1)}, bf16[2064,288]{1,0:T(8,128)(2,1)}, u32[]{:S(2)}) copy-start(bf16[2064,288]{1,0:T(8,128)(2,1)} %copy.114) | copy-start | bytes 3566596
  542.2 42.5 %copy-start.45 = (bf16[288,1152]{1,0:T(8,128)(2,1)S(1)}, bf16[288,1152]{1,0:T(8,128)(2,1)}, u32[]{:S(2)}) copy-start(bf16[288,1152]{1,0:T(8,128)(2,1)} %param.38) | copy-start | bytes 1990660
  544.8 200.1 %reduce-scatter.24.cloned.1.call-start = ((), (), s32[]{:S(2)}) async-start(), calls=%async_computation.14 | async-start | bytes 6266880
  694.9 52.6 %copy-start.27 = (f32[2064]{0:T(1024)S(1)}, f32[2064]{0:T(1024)}, u32[]{:S(2)}) copy-start(f32[2064]{0:T(1024)} %copy-done.26) | copy-start | bytes 24772
  694.9 52.6 %copy-start.29 = (f32[2064]{0:T(1024)S(1)}, f32[2064]{0:T(1024)}, u32[]{:S(2)}) copy-start(f32[2064]{0:T(1024)} %copy-done.28) | copy-start | bytes 24772
  694.9 52.6 %copy-start.31 = (f32[288]{0:T(512)S(1)}, f32[288]{0:T(512)}, u32[]{:S(2)}) copy-start(f32[288]{0:T(512)} %param.34) | copy-start | bytes 3460
  694.9 52.6 %copy-start.34 = (f32[288]{0:T(512)S(1)}, f32[288]{0:T(512)}, u32[]{:S(2)}) copy-start(f32[288]{0:T(512)} %param.35) | copy-start | bytes 3460
  694.9 67.5 %copy-start.4 = (bf16[288,2064]{0,1:T(8,128)(2,1)S(1)}, bf16[288,2064]{0,1:T(8,128)(2,1)}, u32[]{:S(2)}) copy-start(bf16[288,2064]{0,1:T(8,128)(2,1)} %get-tuple-element.203) | copy-start | bytes 3566596
  694.9 115.0 %all-gather.14.cloned.1.call-start = ((), (), s32[]{:S(2)}) async-start(), calls=%async_computation.9 | async-start | bytes 6266880 | tf_op jit(solution)/shard_map/all_gather | solution.py:57
  770.1 343.8 %all-reduce.8.cloned.1.call-start = ((), (), s32[]{:S(2)}) async-start(), calls=%async_computation.15 | async-start | bytes 18579456 | tf_op jit(solution)/shard_map/psum | solution.py:261
  770.1 23.9 %slice-start.2 = ((s8[5013504]{0:T(1024)(128)(4,1)}), s8[4194304]{0:T(1024)(128)(4,1)S(1)}, s32[]{:S(2)}) async-start(s8[5013504]{0:T(1024)(128)(4,1)} %bitcast.211), calls=%async_computation.18 | async-start | bytes 8388608
  770.1 26.8 %slice-start = ((s8[5013504]{0:T(1024)(128)(4,1)}), s8[4194304]{0:T(1024)(128)(4,1)S(1)}, s32[]{:S(2)}) async-start(s8[5013504]{0:T(1024)(128)(4,1)} %bitcast.209), calls=%async_computation.16 | async-start | bytes 8388608
  781.6 15.3 %slice-start.1 = ((s8[5013504]{0:T(1024)(128)(4,1)}), s8[819200]{0:T(1024)(128)(4,1)S(1)}, s32[]{:S(2)}) async-start(s8[5013504]{0:T(1024)(128)(4,1)} %bitcast.209), calls=%async_computation.17 | async-start | bytes 1638400
  819.5 47.6 %copy-start.22 = (bf16[288,1152]{1,0:T(8,128)(2,1)S(1)}, bf16[288,1152]{1,0:T(8,128)(2,1)}, u32[]{:S(2)}) copy-start(bf16[288,1152]{1,0:T(8,128)(2,1)} %param.32) | copy-start | bytes 1990660
  (34 other events, 156.8 us)
Sparse Core Ops, SparseCore 0:
  19.0 84.3 reduce-scatter.15
  126.5 39.6 all-gather.5
  250.5 49.8 reduce-scatter.17
  324.2 39.6 all-gather.7
  365.9 39.0 all-gather.9
  415.4 49.8 reduce-scatter.19
  468.4 49.8 reduce-scatter.21
  545.0 39.6 all-gather.11
  695.0 49.8 reduce-scatter.23
  770.2 39.7 all-gather.13
  818.3 295.5 all-reduce.7
where the time goes:
time: 1140 us
  waiting for transfers between devices  601 us (53%)
  matrix products  221 us (19%)
  local copies, waits for them, and re-layouts  152 us (13%)
  blocking collectives  80.5 us (7%)
  other arithmetic  64.8 us (6%)
  between operations  15.4 us (1%)
    unnamed x16, waiting for transfers between devices  249 us
    psum x1, waiting for transfers between devices, body(): lax.psum(g_w_main.astype(jnp.bfloat16), 'dp').astype(jnp.float32)  236 us
    all_gather x2, waiting for transfers between devices, layer_norm(): return (normed, rstd, lax.all_gather(rounded, 'tp', axis=0, tiled=True))  69.8 us
    unnamed x123, local copies, waits for them, and re-layouts  63.8 us
    all_gather x3, waiting for transfers between devices, fold_back(): piece = lax.all_gather(shard, 'tp', axis=0, tiled=True)  46 us
    psum x1, blocking collectives, body(): lax.psum(g_b_skip.astype(jnp.bfloat16), 'dp').astype(jnp.float32)  39.2 us
    dot_general x4, matrix products, fold_back(): jnp.einsum('fc,ct->ft', weight, piece, preferred_element_type=jnp.float32)  32.7 us
    dot_general x1, matrix products, body(): jnp.einsum('dc,dt->ct', w_up, full_two, preferred_element_type=jnp.float32)  32.2 us
  transfers between devices with their start and end apart: 11, of which 10 were waited for; matrix products, arithmetic and copies ran while one was open for 13% of the time, Pallas kernels for 0%

commit v1 on v0

--- a/solution.py
+++ b/solution.py
@@ -10,6 +10,19 @@
 EPSILON = 1e-06
 ROOT_HALF = 0.7071067811865476
 DENSITY_SCALE = 0.3989422804014327
+
+
+def gather_around(value, axis, dim):
+    ways = lax.axis_size(axis)
+    up = [(d, (d + 1) % ways) for d in range(ways)]
+    down = [(d, (d - 1) % ways) for d in range(ways)]
+    earlier, later = ([value], [value])
+    for _ in range(ways // 2):
+        earlier.append(lax.ppermute(earlier[-1], axis, up))
+    for _ in range((ways - 1) // 2):
+        later.append(lax.ppermute(later[-1], axis, down))
+    line = jnp.concatenate([*earlier[::-1], *later[1:]], axis=dim)
+    return jnp.roll(line, (lax.axis_index(axis) - ways // 2) * value.shape[dim], axis=dim)
 
 
 def item_factors(timesteps, loss_codes, code_weights, group_items):
@@ -54,7 +67,7 @@
 
 
 def fold_back(shard, pairs):
-    piece = lax.all_gather(shard, "tp", axis=0, tiled=True)
+    piece = gather_around(shard, "tp", 0)
     new_acts = tuple(
         (
             jnp.einsum("fc,ct->ft", weight, piece, preferred_element_type=jnp.float32)

time: 1140 us -> 1270 us (1.11)
  local copies, waits for them, and re-layouts: 152 us -> 204 us
  waiting for transfers between devices: 601 us -> 652 us
    ppermute x0 -> x9, waiting for transfers between devices: none -> 113 us  [the longest x6 102 us: gather_around(): earlier.append(lax.ppermute(earlier[-1], axis, up))]
    all_gather x3 -> x0, waiting for transfers between devices: 46 us -> none  [fold_back(): piece = lax.all_gather(shard, 'tp', axis=0, tiled=True)]
    concatenate x0 -> x3, local copies, waits for them, and re-layouts: none -> 29 us  [gather_around(): line = jnp.concatenate([*earlier[::-1], *later[1:]], axis=dim)]
    unnamed x16 -> x13, waiting for transfers between devices: 249 us -> 221 us
    ppermute x0 -> x9, local copies, waits for them, and re-layouts: none -> 23.3 us  [the longest x6 15.5 us: gather_around(): earlier.append(lax.ppermute(earlier[-1], axis, up))]
    unnamed x123 -> x143, local copies, waits for them, and re-layouts: 63.8 us -> 64.7 us
  transfers between devices with their start and end apart: 11 -> 17, of which waited for: 10 -> 13; matrix products, arithmetic and copies ran while one was open for 13% -> 10% of each run, Pallas kernels for 0% -> 0%
where the time goes in v1:
time: 1270 us; the launch traced here: 1260 us
  waiting for transfers between devices  652 us (51%)
  matrix products  225 us (18%)
  local copies, waits for them, and re-layouts  204 us (16%)
  blocking collectives  80.8 us (6%)
  other arithmetic  72.3 us (6%)
  between operations  15.6 us (1%)
    psum x1, waiting for transfers between devices, body(): lax.psum(g_w_main.astype(jnp.bfloat16), 'dp').astype(jnp.float32)  239 us
    unnamed x13, waiting for transfers between devices  221 us
    ppermute x6, waiting for transfers between devices, gather_around(): earlier.append(lax.ppermute(earlier[-1], axis, up))  102 us
    all_gather x2, waiting for transfers between devices, layer_norm(): return (normed, rstd, lax.all_gather(rounded, 'tp', axis=0, tiled=True))  79.3 us
    unnamed x143, local copies, waits for them, and re-layouts  64.7 us
    psum x1, blocking collectives, body(): lax.psum(g_b_skip.astype(jnp.bfloat16), 'dp').astype(jnp.float32)  39.7 us
    dot_general x1, matrix products, body(): jnp.einsum('dc,dt->ct', w_up, full_two, preferred_element_type=jnp.float32)  32.7 us
    dot_general x4, matrix products, fold_back(): jnp.einsum('fc,ct->ft', weight, piece, preferred_element_type=jnp.float32)  31.8 us
  transfers between devices with their start and end apart: 17, of which 13 were waited for; matrix products, arithmetic and copies ran while one was open for 10% of the time, Pallas kernels for 0%

profile of v1, /device:TPU:0, one launch (start us, length us, event | category | flops | bytes accessed | tf_op | source)
XLA Modules:
  0.0 1255.8 jit_solution(4794294259096169880)
XLA Ops:
  18.9 84.4 %reduce-scatter.16.cloned.1.call-done = f32[288,2064]{1,0:T(8,128)} async-done(((f32[1152,2064]{1,0:T(8,128)}), f32[288,2064]{1,0:T(8,128)}) %reduce-scatter.16.cloned.1.call-update) | async-done | bytes 2377744
  109.4 10.3 all-reduce.3
  126.6 39.6 %all-gather.3.cloned.1.call-done = bf16[1152,2064]{1,0:T(8,128)(2,1)} async-done(((bf16[288,2064]{1,0:T(8,128)(2,1)}), bf16[1152,2064]{1,0:T(8,128)(2,1)}) %all-gather.3.cloned.1.call-update) | async-done | bytes 4755472 | tf_op jit(solution)/shard_map/all_gather | solution.py:48
  202.9 23.2 %while.26 = (s32[]{:T(128)}, bf16[4,4,72,2,258]{4,2,3,1,0:T(8,128)(2,1)}, f32[4,4,2,258]{3,2,1,0:T(2,128)}, bf16[4,4,72,2,258]{4,2,3,1,0:T(8,128)(2,1)}, bf16[4,...) while((s32[]{:T(128)}, bf16[4,4,72,2,258]{4,2,3,1,0:T(8,128)(2,1)}, ...), condition=%wide.region_8.0_spmd, body=%wide.region_5.8_spmd.sunk | while | flops 157770096 | bytes 8231833 | solution.py:187
  250.2 50.0 %reduce-scatter.18.cloned.1.call-done = bf16[288,2064]{1,0:T(8,128)(2,1)} async-done(((bf16[1152,2064]{1,0:T(8,128)(2,1)}), bf16[288,2064]{1,0:T(8,128)(2,1)}) %reduce-scatter.18.cloned.1.call-update) | async-done | bytes 1188880
  307.4 10.3 all-reduce.2
  324.5 39.8 %all-gather.5.cloned.1.call-done = bf16[1152,2064]{1,0:T(8,128)(2,1)} async-done(((bf16[288,2064]{1,0:T(8,128)(2,1)}), bf16[1152,2064]{1,0:T(8,128)(2,1)}) %all-gather.5.cloned.1.call-update) | async-done | bytes 4755472 | tf_op jit(solution)/shard_map/all_gather | solution.py:48
  364.2 32.7 %fusion.68 = (bf16[1152,2064]{0,1:T(8,128)(2,1)S(1)}, f32[1152,2064]{0,1:T(8,128)}) fusion(f32[1152]{0:T(1024)S(1)} %copy-done.56, bf16[1152,2064]{1,0:T(8,128)(2,1)} %all-gather.5.cloned.1.call-done, bf16[1152,1152]{1,0:T(8,128)(2,1)S(1)} %copy-done), kind=kOutput, calls=%fused_computation.81 | convolution fusion | flops 5635215360 | bytes 21680640 | tf_op jit(solution)/shard_map/dc,dt->ct/dot_general | solution.py:201
  399.2 8.5 fusion.63
  407.7 8.4 copy.143
  427.2 44.2 %collective-permute-done = bf16[288,2064]{1,0:T(8,128)(2,1)} collective-permute-done((bf16[288,2064]{1,0:T(8,128)(2,1)}, bf16[288,2064]{1,0:T(8,128)(2,1)}, u32[]{:S(2)}, u32[]{:S(2)}) %collective-permute-start) | collective-permute-done | bytes 1188896 | tf_op jit(solution)/shard_map/ppermute | solution.py:21
  476.6 19.3 %collective-permute-done.1 = bf16[288,2064]{1,0:T(8,128)(2,1)} collective-permute-done((bf16[288,2064]{1,0:T(8,128)(2,1)}, bf16[288,2064]{1,0:T(8,128)(2,1)}, u32[]{:S(2)}, u32[]{:S(2)}) %collective-permute-start.1) | collective-permute-done | bytes 1188896 | tf_op jit(solution)/shard_map/ppermute | solution.py:21
  498.5 9.8 concatenate.12
  508.4 15.2 %fusion.129 = (bf16[1152]{0:T(1024)(128)(2,1)}, bf16[1152,2064]{0,1:T(8,128)(2,1)S(1)}) fusion(f32[1152,2064]{0,1:T(8,128)} %get-tuple-element.221, bf16[1152,1152]{1,0:T(8,128)(2,1)} %param.46, s32[]{:T(128)S(6)} %select_n.15, bf16[1152,2064]{0,1:T(8,128)(2,1)} %concatenate.12), kind=kOutput, calls=%fused_computation.185 | convolution fusion | flops 5513950208 | bytes 21678340 | tf_op jit(solution)/shard_map/fc,ct->ft/dot_general | solution.py:73
  525.8 8.7 fusion.64
  534.5 8.4 copy.145
  545.8 47.3 %reduce-scatter.22.cloned.1.call-done = bf16[288,2064]{1,0:T(8,128)(2,1)} async-done(((bf16[1152,2064]{1,0:T(8,128)(2,1)}), bf16[288,2064]{1,0:T(8,128)(2,1)}) %reduce-scatter.22.cloned.1.call-update) | async-done | bytes 1188880
  602.2 10.3 all-reduce.1
  621.3 27.0 %collective-permute-done.3 = bf16[288,2064]{1,0:T(8,128)(2,1)} collective-permute-done((bf16[288,2064]{1,0:T(8,128)(2,1)}, bf16[288,2064]{1,0:T(8,128)(2,1)}, u32[]{:S(2)}, u32[]{:S(2)}) %collective-permute-start.3) | collective-permute-done | bytes 1188896 | tf_op jit(solution)/shard_map/ppermute | solution.py:21
  653.8 11.5 collective-permute-done.4
  667.9 9.6 concatenate.13
  696.5 51.8 %while.27 = (s32[]{:T(128)}, bf16[4,4,72,2,258]{4,2,3,1,0:T(8,128)(2,1)}, bf16[4,4,72,2,258]{4,2,3,1,0:T(8,128)(2,1)}, bf16[4,4,72,2,258]{4,2,3,1,0:T(8,128)(2,1...) while((s32[]{:T(128)}, ...), condition=%wide.region_23.25_spmd, body=%wide.region_21.24_spmd.sunk | while | flops 390539744 | bytes 20462064 | solution.py:240
  781.8 8.4 copy.147
  790.3 11.4 convolution_convert_fusion.4
  801.7 39.0 %reduce-scatter.24.cloned.1.call-done = bf16[288,2064]{1,0:T(8,128)(2,1)} async-done(((bf16[1152,2064]{1,0:T(8,128)(2,1)}), bf16[288,2064]{1,0:T(8,128)(2,1)}) %reduce-scatter.24.cloned.1.call-update) | async-done | bytes 1188880
  847.6 10.3 all-reduce
  865.6 14.8 %convolution_convert_fusion.3 = bf16[1152,1152]{1,0:T(8,128)(2,1)} fusion(bf16[1152,2064]{0,1:T(8,128)(2,1)} %copy-done.60, s32[]{:T(128)S(6)} %select_n.15, bf16[1152,2064]{0,1:T(8,128)(2,1)} %concatenate.12), kind=kOutput, calls=%fused_computation.107 | convolution fusion | flops 5489123328 | bytes 12165124 | tf_op jit(solution)/shard_map/ft,ct->fc/dot_general | solution.py:79
  887.2 9.3 fusion.111
  899.1 10.2 collective-permute-done.8
  914.5 9.5 concatenate.14
  942.1 39.7 %all-reduce.4 = (bf16[288]{0:T(512)(128)(2,1)S(1)}, bf16[288]{0:T(512)(128)(2,1)S(1)}, bf16[288]{0:T(512)(128)(2,1)S(1)}, bf16[288]{0:T(512)(128)(2,1)S(1)}, bf1...) all-reduce(bf16[288]{0:T(512)(128)(2,1)S(1)} %get-tuple-element.205, ...), channel_id=1, replica_groups=mesh['dp'=8,'tp'=4] {'dp'}, use_global_device_ids=true, to_apply=%region_32.34 | all-reduce | flops 3168 | bytes 12672 | tf_op jit(solution)/shard_map/psum | solution.py:276
  995.4 239.0 %all-reduce.8.cloned.1.call-done = (bf16[288,1152]{1,0:T(8,128)(2,1)}, bf16[288,1152]{1,0:T(8,128)(2,1)}, bf16[3,1152,288]{1,2,0:T(8,128)(2,1)}, bf16[288,1152]{...) async-done(((bf16[288,1152]{1,0:T(8,128)(2,1)}, bf16[288,1152]{1,0:T(8,128)(2,1)}, bf16[3,1152,288]{1,2,0:T(8,128)(2,1)}, ...) | async-done | bytes 9289744 | tf_op jit(solution)/shard_map/psum | solution.py:274
  (301 shorter events, 352.7 us)
Async XLA Ops:
  7.2 357.0 %copy-start = (bf16[1152,1152]{1,0:T(8,128)(2,1)S(1)}, bf16[1152,1152]{1,0:T(8,128)(2,1)}, u32[]{:S(2)}) copy-start(bf16[1152,1152]{1,0:T(8,128)(2,1)} %param.44) | copy-start | bytes 7962628
  7.2 96.1 %reduce-scatter.16.cloned.1.call-start = ((), (), s32[]{:S(2)}) async-start(), calls=%async_computation.7 | async-start | bytes 12533760
  18.8 88.1 %copy-start.38 = (f32[288]{0:T(512)S(1)}, f32[288]{0:T(512)}, u32[]{:S(2)}) copy-start(f32[288]{0:T(512)} %param.36) | copy-start | bytes 3460
  18.8 101.5 %copy-start.42 = (f32[288]{0:T(512)S(1)}, f32[288]{0:T(512)}, u32[]{:S(2)}) copy-start(f32[288]{0:T(512)} %param.37) | copy-start | bytes 3460
  18.8 101.5 %copy-start.47 = (f32[288]{0:T(512)S(1)}, f32[288]{0:T(512)}, u32[]{:S(2)}) copy-start(f32[288]{0:T(512)} %param.38) | copy-start | bytes 3460
  18.8 147.4 %all-gather.3.cloned.1.call-start = ((), (), s32[]{:S(2)}) async-start(), calls=%async_computation.5 | async-start | bytes 6266880 | tf_op jit(solution)/shard_map/all_gather | solution.py:48
  126.4 173.8 %reduce-scatter.18.cloned.1.call-start = ((), (), s32[]{:S(2)}) async-start(), calls=%async_computation.8 | async-start | bytes 6266880
  250.2 52.6 %copy-start.48 = (f32[288]{0:T(512)S(1)}, f32[288]{0:T(512)}, u32[]{:S(2)}) copy-start(f32[288]{0:T(512)} %param.41) | copy-start | bytes 3460
  250.2 114.0 %all-gather.5.cloned.1.call-start = ((), (), s32[]{:S(2)}) async-start(), calls=%async_computation.6 | async-start | bytes 6266880 | tf_op jit(solution)/shard_map/all_gather | solution.py:48
  324.4 218.8 %reduce-scatter.20.cloned.1.call-start = ((), (), s32[]{:S(2)}) async-start(), calls=%async_computation.9 | async-start | bytes 6266880
  416.1 177.0 %reduce-scatter.22.cloned.1.call-start = ((), (), s32[]{:S(2)}) async-start(), calls=%async_computation.10 | async-start | bytes 6266880
  417.2 195.2 %copy-start.28 = (f32[2064]{0:T(1024)}, f32[2064]{0:T(1024)S(1)}, u32[]{:S(2)}) copy-start(f32[2064]{0:T(1024)S(1)} %mul.229) | copy-start | bytes 24772
  425.5 46.0 %collective-permute-start = (bf16[288,2064]{1,0:T(8,128)(2,1)}, bf16[288,2064]{1,0:T(8,128)(2,1)}, u32[]{:S(2)}, u32[]{:S(2)}) collective-permute-start(bf16[288,2064]{1,0:T(8,128)(2,1)} %copy.115), channel_id=1, source_target_pairs={{0,1},{1,2},{2,3},{3,0},{4,5},{5,6},{6,7},{7,4},{8,9},{9,10},{10,1... | collective-permute-start | bytes 3566600 | tf_op jit(solution)/shard_map/ppermute | solution.py:21
  425.7 48.3 %collective-permute-start.2 = (bf16[288,2064]{1,0:T(8,128)(2,1)}, bf16[288,2064]{1,0:T(8,128)(2,1)}, u32[]{:S(2)}, u32[]{:S(2)}) collective-permute-start(bf16[288,2064]{1,0:T(8,128)(2,1)} %copy.115), channel_id=1, source_target_pairs={{0,3},{1,0},{2,1},{3,2},{4,7},{5,4},{6,5},{7,6},{8,11},{9,8},{10,9... | collective-permute-start | bytes 3566600 | tf_op jit(solution)/shard_map/ppermute | solution.py:23
  471.4 24.5 %collective-permute-start.1 = (bf16[288,2064]{1,0:T(8,128)(2,1)}, bf16[288,2064]{1,0:T(8,128)(2,1)}, u32[]{:S(2)}, u32[]{:S(2)}) collective-permute-start(bf16[288,2064]{1,0:T(8,128)(2,1)} %collective-permute-done), channel_id=1, source_target_pairs={{0,1},{1,2},{2,3},{3,0},{4,5},{5,6},{6,7},{7,4},{8,9},{9,10},{10,1... | collective-permute-start | bytes 3566600 | tf_op jit(solution)/shard_map/ppermute | solution.py:21
  542.9 52.8 %copy-start.35 = (f32[2064]{0:T(1024)S(1)}, f32[2064]{0:T(1024)}, u32[]{:S(2)}) copy-start(f32[2064]{0:T(1024)} %copy-done.34) | copy-start | bytes 24772
  542.9 52.8 %copy-start.37 = (f32[2064]{0:T(1024)S(1)}, f32[2064]{0:T(1024)}, u32[]{:S(2)}) copy-start(f32[2064]{0:T(1024)} %copy-done.36) | copy-start | bytes 24772
  542.9 52.8 %copy-start.41 = (f32[288]{0:T(512)S(1)}, f32[288]{0:T(512)}, u32[]{:S(2)}) copy-start(f32[288]{0:T(512)} %param.42) | copy-start | bytes 3460
  542.9 52.8 %copy-start.50 = (f32[288]{0:T(512)S(1)}, f32[288]{0:T(512)}, u32[]{:S(2)}) copy-start(f32[288]{0:T(512)} %param.47) | copy-start | bytes 3460
  542.9 297.7 %reduce-scatter.24.cloned.1.call-start = ((), (), s32[]{:S(2)}) async-start(), calls=%async_computation.11 | async-start | bytes 6266880
  619.6 28.8 %collective-permute-start.3 = (bf16[288,2064]{1,0:T(8,128)(2,1)}, bf16[288,2064]{1,0:T(8,128)(2,1)}, u32[]{:S(2)}, u32[]{:S(2)}) collective-permute-start(bf16[288,2064]{1,0:T(8,128)(2,1)} %copy.120), channel_id=1, source_target_pairs={{0,1},{1,2},{2,3},{3,0},{4,5},{5,6},{6,7},{7,4},{8,9},{9,10},{10,1... | collective-permute-start | bytes 3566600 | tf_op jit(solution)/shard_map/ppermute | solution.py:21
  619.6 31.6 %collective-permute-start.5 = (bf16[288,2064]{1,0:T(8,128)(2,1)}, bf16[288,2064]{1,0:T(8,128)(2,1)}, u32[]{:S(2)}, u32[]{:S(2)}) collective-permute-start(bf16[288,2064]{1,0:T(8,128)(2,1)} %copy.120), channel_id=1, source_target_pairs={{0,3},{1,0},{2,1},{3,2},{4,7},{5,4},{6,5},{7,6},{8,11},{9,8},{10,9... | collective-permute-start | bytes 3566600 | tf_op jit(solution)/shard_map/ppermute | solution.py:23
  648.3 16.9 %collective-permute-start.4 = (bf16[288,2064]{1,0:T(8,128)(2,1)}, bf16[288,2064]{1,0:T(8,128)(2,1)}, u32[]{:S(2)}, u32[]{:S(2)}) collective-permute-start(bf16[288,2064]{1,0:T(8,128)(2,1)} %collective-permute-done.3), channel_id=1, source_target_pairs={{0,1},{1,2},{2,3},{3,0},{4,5},{5,6},{6,7},{7,4},{8,9},{9,10},{10,1... | collective-permute-start | bytes 3566600 | tf_op jit(solution)/shard_map/ppermute | solution.py:21
  790.2 53.0 %copy-start.31 = (f32[2064]{0:T(1024)S(1)}, f32[2064]{0:T(1024)}, u32[]{:S(2)}) copy-start(f32[2064]{0:T(1024)} %copy-done.30) | copy-start | bytes 24772
  790.2 53.0 %copy-start.33 = (f32[2064]{0:T(1024)S(1)}, f32[2064]{0:T(1024)}, u32[]{:S(2)}) copy-start(f32[2064]{0:T(1024)} %copy-done.32) | copy-start | bytes 24772
  790.2 53.0 %copy-start.39 = (f32[288]{0:T(512)S(1)}, f32[288]{0:T(512)}, u32[]{:S(2)}) copy-start(f32[288]{0:T(512)} %param.36) | copy-start | bytes 3460
  790.2 53.0 %copy-start.43 = (f32[288]{0:T(512)S(1)}, f32[288]{0:T(512)}, u32[]{:S(2)}) copy-start(f32[288]{0:T(512)} %param.37) | copy-start | bytes 3460
  790.2 444.1 %all-reduce.8.cloned.1.call-start = ((), (), s32[]{:S(2)}) async-start(), calls=%async_computation.12 | async-start | bytes 18579456 | tf_op jit(solution)/shard_map/psum | solution.py:274
  801.7 56.2 %copy-start.3 = (bf16[288,2064]{0,1:T(8,128)(2,1)S(1)}, bf16[288,2064]{0,1:T(8,128)(2,1)}, u32[]{:S(2)}) copy-start(bf16[288,2064]{0,1:T(8,128)(2,1)} %copy-done.2) | copy-start | bytes 3566596
  865.6 16.7 %collective-permute-start.6 = (bf16[288,2064]{1,0:T(8,128)(2,1)}, bf16[288,2064]{1,0:T(8,128)(2,1)}, u32[]{:S(2)}, u32[]{:S(2)}) collective-permute-start(bf16[288,2064]{1,0:T(8,128)(2,1)} %copy.129), channel_id=1, source_target_pairs={{0,1},{1,2},{2,3},{3,0},{4,5},{5,6},{6,7},{7,4},{8,9},{9,10},{10,1... | collective-permute-start | bytes 3566600 | tf_op jit(solution)/shard_map/ppermute | solution.py:21
  880.4 29.0 %collective-permute-start.8 = (bf16[288,2064]{1,0:T(8,128)(2,1)}, bf16[288,2064]{1,0:T(8,128)(2,1)}, u32[]{:S(2)}, u32[]{:S(2)}) collective-permute-start(bf16[288,2064]{1,0:T(8,128)(2,1)} %copy.129), channel_id=1, source_target_pairs={{0,3},{1,0},{2,1},{3,2},{4,7},{5,4},{6,5},{7,6},{8,11},{9,8},{10,9... | collective-permute-start | bytes 3566600 | tf_op jit(solution)/shard_map/ppermute | solution.py:23
  882.3 29.7 %collective-permute-start.7 = (bf16[288,2064]{1,0:T(8,128)(2,1)}, bf16[288,2064]{1,0:T(8,128)(2,1)}, u32[]{:S(2)}, u32[]{:S(2)}) collective-permute-start(bf16[288,2064]{1,0:T(8,128)(2,1)} %collective-permute-done.6), channel_id=1, source_target_pairs={{0,1},{1,2},{2,3},{3,0},{4,5},{5,6},{6,7},{7,4},{8,9},{9,10},{10,1... | collective-permute-start | bytes 3566600 | tf_op jit(solution)/shard_map/ppermute | solution.py:21
  (50 other events, 422.2 us)
Sparse Core Ops, SparseCore 0:
  18.9 84.3 reduce-scatter.15
  126.5 39.6 all-gather.2
  250.3 49.8 reduce-scatter.17
  324.5 39.6 all-gather.4
  416.2 71.5 reduce-scatter.19
  543.0 50.0 reduce-scatter.21
  790.3 50.2 reduce-scatter.23
  936.9 297.4 all-reduce.7
